TPU v7x, 32 devices: a 4x4x1 block of a 4x4x8 slice. The times are simulated.
32 devices in a mesh: dp: 1 (over z), tp: 4 (over y), cp: 8 (over x, core).
Axes of the slice: x: 4, y: 4, z: 1, core: 2. Of those that a mesh axis runs over, the one named last changes fastest.
The devices are a block of a 4x4x8 slice.
Arguments:
- x: bfloat16 [8192, 5376], P(('dp', 'cp', 'tp'))
- w_q: bfloat16 [5376, 4096], P(None, 'tp')
- w_k: bfloat16 [5376, 2048], P(None, 'tp')
- w_v: bfloat16 [5376, 2048], P(None, 'tp')
- w_o: bfloat16 [4096, 5376], P('tp')
Outputs:
- output: bfloat16 [8192, 5376], P(('dp', 'cp', 'tp'))
All inputs are finite; a program needn't handle non-finite values.
Results may differ from a plain program's by a relative error of at most 0.00599733.
Values are sent between devices in bfloat16 or wider.
A program may use at most 768 MiB of HBM per device.

v0:
```python
import jax
import jax.numpy as jnp
from jax import lax
from jax.sharding import PartitionSpec as P

HEAD_DIM = 128


def block_scores(q_part, k_part):
    raw_scores = jnp.einsum("qhge,khe->hgqk", q_part, k_part, preferred_element_type=jnp.float32)
    return raw_scores * (HEAD_DIM ** -0.5)


def merge_block(soft_state, scores, v_part):
    run_max, run_sum, run_acc = soft_state
    new_max = jnp.maximum(run_max, scores.max(axis=-1))
    rescale = jnp.exp(run_max - new_max)
    p_block = jnp.exp(scores - new_max[..., None])
    new_sum = run_sum * rescale + p_block.sum(axis=-1)
    new_acc = run_acc * rescale[..., None] + jnp.einsum("hgqk,khe->hgqe", p_block.astype(jnp.bfloat16), v_part, preferred_element_type=jnp.float32)
    return new_max, new_sum, new_acc


def solution(mesh):
    cp_size = mesh.shape["cp"]
    row_spec = P(("dp", "cp", "tp"), None)

    def local_layer(x_loc, w_q, w_k, w_v, w_o):
        model_width = x_loc.shape[1]
        kv_local = w_k.shape[1] // HEAD_DIM
        group_size = w_q.shape[1] // w_k.shape[1]
        x_block = lax.all_gather(x_loc, "tp", axis=0, tiled=True)
        piece_len = x_block.shape[0] // 2
        q_all = jnp.dot(x_block, w_q, preferred_element_type=jnp.float32).astype(jnp.bfloat16).reshape(2, piece_len, kv_local, group_size, HEAD_DIM)
        k_all = jnp.dot(x_block, w_k, preferred_element_type=jnp.float32).astype(jnp.bfloat16).reshape(2, piece_len, kv_local, HEAD_DIM)
        v_all = jnp.dot(x_block, w_v, preferred_element_type=jnp.float32).astype(jnp.bfloat16).reshape(2, piece_len, kv_local, HEAD_DIM)
        q_low = q_all[0]
        q_high = q_all[1]
        cp_rank = lax.axis_index("cp")
        offsets = jnp.arange(piece_len)
        pos_low = cp_rank * piece_len + offsets
        pos_high = (2 * cp_size - 1 - cp_rank) * piece_len + offsets
        pos_both = jnp.concatenate([pos_low, pos_high])
        stat_shape = (kv_local, group_size, piece_len)
        empty_state = (jnp.full(stat_shape, -jnp.inf, jnp.float32), jnp.zeros(stat_shape, jnp.float32), jnp.zeros(stat_shape + (HEAD_DIM,), jnp.float32))
        k_flat = k_all.reshape(2 * piece_len, kv_local, HEAD_DIM)
        v_flat = v_all.reshape(2 * piece_len, kv_local, HEAD_DIM)
        low_scores = jnp.where(pos_low[:, None] >= pos_low[None, :], block_scores(q_low, k_all[0]), -jnp.inf)
        high_scores = jnp.where(pos_high[:, None] >= pos_both[None, :], block_scores(q_high, k_flat), -jnp.inf)
        own_states = (merge_block(empty_state, low_scores, v_all[0]), merge_block(empty_state, high_scores, v_flat))

        def earlier_source(states, kv_src):
            state_low, state_high = states
            k_src = kv_src[0, 0]
            v_src = kv_src[1, 0]
            return (merge_block(state_low, block_scores(q_low, k_src), v_src), merge_block(state_high, block_scores(q_high, k_src), v_src))

        def later_source(states, kv_src):
            state_low, state_high = states
            k_src = kv_src[0].reshape(2 * piece_len, kv_local, HEAD_DIM)
            v_src = kv_src[1].reshape(2 * piece_len, kv_local, HEAD_DIM)
            return (state_low, merge_block(state_high, block_scores(q_high, k_src), v_src))

        shift_pairs = [(dev_idx, (dev_idx + 1) % cp_size) for dev_idx in range(cp_size)]

        def kv_step(step_idx, loop_carry):
            states, kv_held = loop_carry
            kv_held = lax.ppermute(kv_held, "cp", shift_pairs)
            source = (cp_rank - step_idx) % cp_size
            states = lax.cond(source < cp_rank, earlier_source, later_source, states, kv_held)
            return states, kv_held

        kv_pair = jnp.stack([k_all, v_all])
        final_carry = lax.fori_loop(1, cp_size, kv_step, (own_states, kv_pair))
        state_low, state_high = final_carry[0]
        out_low = (state_low[2] / state_low[1][..., None]).astype(jnp.bfloat16)
        out_high = (state_high[2] / state_high[1][..., None]).astype(jnp.bfloat16)
        attn_out = jnp.stack([out_low, out_high], axis=2)
        w_o_heads = w_o.reshape(kv_local, group_size, HEAD_DIM, model_width)
        partial = jnp.einsum("hgsqe,hged->sqd", attn_out, w_o_heads, preferred_element_type=jnp.float32).reshape(2 * piece_len, model_width)
        y_loc = lax.psum_scatter(partial, "tp", scatter_dimension=0, tiled=True)
        return y_loc.astype(jnp.bfloat16)

    return jax.shard_map(local_layer, mesh=mesh, in_specs=(row_spec, P(None, "tp"), P(None, "tp"), P(None, "tp"), P("tp", None)), out_specs=row_spec, check_vma=False)
```

profile of v0, /device:TPU:97, one launch (start us, length us, event | category | flops | bytes accessed | tf_op | source)
XLA Modules:
  0.0 820.5 jit_solution(9443931132807175968)
XLA Ops:
  8.0 107.8 %all-gather.2.cloned.1.call-done = bf16[1024,5376]{1,0:T(8,128)(2,1)} async-done(((bf16[256,5376]{1,0:T(8,128)(2,1)}), bf16[1024,5376]{1,0:T(8,128)(2,1)}) %all-gather.2.cloned.1.call-update) | async-done | bytes 11010064 | tf_op jit(solution)/shard_map/all_gather | solution.py:32
  115.8 10.3 %convolution_convert_fusion.1 = bf16[1024,512]{0,1:T(8,128)(2,1)S(1)} fusion(bf16[1024,5376]{1,0:T(8,128)(2,1)} %all-gather.2.cloned.1.call-done, bf16[5376,512]{1,0:T(8,128)(2,1)} %param.12), kind=kOutput, calls=%fused_computation.72 | convolution fusion | flops 5637668864 | bytes 17563648 | tf_op jit(solution)/shard_map/dot_general | solution.py:36
  128.8 10.3 %convolution_convert_fusion.2 = bf16[1024,512]{0,1:T(8,128)(2,1)S(1)} fusion(bf16[1024,5376]{1,0:T(8,128)(2,1)} %all-gather.2.cloned.1.call-done, bf16[5376,512]{1,0:T(8,128)(2,1)} %param.11), kind=kOutput, calls=%fused_computation.73 | convolution fusion | flops 5637668864 | bytes 17563648 | tf_op jit(solution)/shard_map/dot_general | solution.py:35
  141.6 15.6 %convolution_convert_fusion = bf16[1024,1024]{0,1:T(8,128)(2,1)S(1)} fusion(bf16[1024,5376]{1,0:T(8,128)(2,1)} %all-gather.2.cloned.1.call-done, bf16[5376,1024]{1,0:T(8,128)(2,1)} %param.10), kind=kOutput, calls=%fused_computation.69 | convolution fusion | flops 11275337728 | bytes 24117248 | tf_op jit(solution)/shard_map/dot_general | solution.py:34
  165.3 8.6 %fusion.42 = (f32[4,2,512]{2,1,0:T(2,128)S(1)}, f32[4,1024,512,2]{2,1,3,0:T(8,128)}) fusion(pred[512,1024]{0,1:T(8,128)(4,1)S(1)} %broadcast_compare_fusion, bf16[1024,4,128,1]{0,2,3,1:T(8,128)(2,1)} %bitcast.173, bf16[512,4,2,128]{0,3,2,1:T(8,128)(2,1)S(1)} %bitcast.168), kind=kOutput, calls=%fused_computation.51 | convolution fusion | flops 1086320640 | bytes 19415040 | tf_op jit(solution)/shard_map/qhge,khe->hgqk/dot_general | solution.py:10
  173.9 9.3 %fusion.41 = f32[4,2,512]{2,1,0:T(2,128)S(1)} fusion(f32[4,1024,512,2]{2,1,3,0:T(8,128)} %get-tuple-element.430, f32[4,2,512]{2,1,0:T(2,128)S(1)} %get-tuple-element.534, pred[512,1024]{0,1:T(8,128)(4,1)S(1)} %broadcast_compare_fusion), kind=kLoop, calls=%fused_computation.49 | loop fusion | flops 16773120 | bytes 17334272 | tf_op jit(solution)/shard_map/reduce_sum | solution.py:19
  196.5 9.6 %fusion.59 = f32[4,2,512,128]{3,2,1,0:T(8,128)} fusion(bf16[1024,4,128,1]{0,2,3,1:T(8,128)(2,1)S(1)} %bitcast.179, f32[4,1024,512,2]{2,1,3,0:T(8,128)} %get-tuple-element.430, f32[4,2,512]{2,1,0:T(2,128)S(1)} %get-tuple-element.534, pred[512,1024]{0,1:T(8,128)(4,1)S(1)} %broadcast_compare_fusion, f32[4,2,512]{2,1,0:T(2,128)S(1)} %get-tuple-element.423), kind=kOutput, calls=%fused_computation.71 | convolution fusion | flops 1091043328 | bytes 20480000 | tf_op jit(solution)/shard_map/hgqk,khe->hgqe/dot_general | solution.py:20
  207.6 372.5 %while.27 = (s32[]{:T(128)}, f32[4,2,512]{2,1,0:T(2,128)S(1)}, f32[4,2,512]{2,1,0:T(2,128)S(1)}, f32[4,2,512,128]{3,2,1,0:T(8,128)}, f32[4,2,512]{2,1,0:T(2,128)...) while((s32[]{:T(128)}, f32[4,2,512]{2,1,0:T(2,128)S(1)}, ...), condition=%wide.region_13.14_spmd, body=%wide.region_4.13_spmd.sunk | while | flops 2183151616 | bytes 96993864 | solution.py:74
  209.8 23.0 %collective-permute-done = bf16[2,2,512,4,128]{4,2,3,1,0:T(8,128)(2,1)S(1)} collective-permute-done((bf16[2,2,512,4,128]{4,2,3,1,0:T(8,128)(2,1)}, bf16[2,2,512,4,128]{4,2,3,1,0:T(8,128)(2,1)S(1)}, u32[]{:S(2)}, u32[]{:S(2)}) %collective-permute-start) | collective-permute-done | bytes 2097184 | tf_op jit(solution)/shard_map/while/body/eval_jaxpr/ppermute | solution.py:68
  232.8 17.1 %conditional.2 = (f32[4,2,512]{2,1,0:T(2,128)S(1)}, f32[4,2,512]{2,1,0:T(2,128)S(1)}, f32[4,2,512,128]{3,2,1,0:T(8,128)}, f32[4,2,512]{2,1,0:T(2,128)}, f32[4,2,...) conditional(s32[]{:T(128)} %convert_element_type.81, (bf16[2,2,512,4,128]{4,2,3,1,0:T(8,128)(2,1)S(1)}, ...), branch_computations={%region_5.7_spmd, %region_8.12_spmd} | conditional | flops 2183151616 | bytes 84377736 | solution.py:70
  254.4 23.0 %collective-permute-done = bf16[2,2,512,4,128]{4,2,3,1,0:T(8,128)(2,1)S(1)} collective-permute-done((bf16[2,2,512,4,128]{4,2,3,1,0:T(8,128)(2,1)}, bf16[2,2,512,4,128]{4,2,3,1,0:T(8,128)(2,1)S(1)}, u32[]{:S(2)}, u32[]{:S(2)}) %collective-permute-start) | collective-permute-done | bytes 2097184 | tf_op jit(solution)/shard_map/while/body/eval_jaxpr/ppermute | solution.py:68
  277.4 27.6 %conditional.2 = (f32[4,2,512]{2,1,0:T(2,128)S(1)}, f32[4,2,512]{2,1,0:T(2,128)S(1)}, f32[4,2,512,128]{3,2,1,0:T(8,128)}, f32[4,2,512]{2,1,0:T(2,128)}, f32[4,2,...) conditional(s32[]{:T(128)} %convert_element_type.81, (bf16[2,2,512,4,128]{4,2,3,1,0:T(8,128)(2,1)S(1)}, ...), branch_computations={%region_5.7_spmd, %region_8.12_spmd} | conditional | flops 2183151616 | bytes 84377736 | solution.py:70
  277.6 8.1 bitcast_reduce_fusion
  286.3 8.7 %fusion.2 = f32[4,2,512]{2,1,0:T(2,128)S(1)} fusion(f32[4,1024,512,2]{2,1,3,0:T(8,128)} %get-tuple-element.414, f32[4,2,512]{2,1,0:T(2,128)} %max.6), kind=kLoop, calls=%fused_computation.4 | loop fusion | flops 12578816 | bytes 16809984 | tf_op jit(solution)/shard_map/while/body/eval_jaxpr/cond/branch_0_fun/reduce_sum | solution.py:19
  307.0 23.0 %collective-permute-done = bf16[2,2,512,4,128]{4,2,3,1,0:T(8,128)(2,1)S(1)} collective-permute-done((bf16[2,2,512,4,128]{4,2,3,1,0:T(8,128)(2,1)}, bf16[2,2,512,4,128]{4,2,3,1,0:T(8,128)(2,1)S(1)}, u32[]{:S(2)}, u32[]{:S(2)}) %collective-permute-start) | collective-permute-done | bytes 2097184 | tf_op jit(solution)/shard_map/while/body/eval_jaxpr/ppermute | solution.py:68
  330.0 27.6 %conditional.2 = (f32[4,2,512]{2,1,0:T(2,128)S(1)}, f32[4,2,512]{2,1,0:T(2,128)S(1)}, f32[4,2,512,128]{3,2,1,0:T(8,128)}, f32[4,2,512]{2,1,0:T(2,128)}, f32[4,2,...) conditional(s32[]{:T(128)} %convert_element_type.81, (bf16[2,2,512,4,128]{4,2,3,1,0:T(8,128)(2,1)S(1)}, ...), branch_computations={%region_5.7_spmd, %region_8.12_spmd} | conditional | flops 2183151616 | bytes 84377736 | solution.py:70
  338.8 8.7 %fusion.2 = f32[4,2,512]{2,1,0:T(2,128)S(1)} fusion(f32[4,1024,512,2]{2,1,3,0:T(8,128)} %get-tuple-element.414, f32[4,2,512]{2,1,0:T(2,128)} %max.6), kind=kLoop, calls=%fused_computation.4 | loop fusion | flops 12578816 | bytes 16809984 | tf_op jit(solution)/shard_map/while/body/eval_jaxpr/cond/branch_0_fun/reduce_sum | solution.py:19
  362.1 23.0 %collective-permute-done = bf16[2,2,512,4,128]{4,2,3,1,0:T(8,128)(2,1)S(1)} collective-permute-done((bf16[2,2,512,4,128]{4,2,3,1,0:T(8,128)(2,1)}, bf16[2,2,512,4,128]{4,2,3,1,0:T(8,128)(2,1)S(1)}, u32[]{:S(2)}, u32[]{:S(2)}) %collective-permute-start) | collective-permute-done | bytes 2097184 | tf_op jit(solution)/shard_map/while/body/eval_jaxpr/ppermute | solution.py:68
  385.0 27.6 %conditional.2 = (f32[4,2,512]{2,1,0:T(2,128)S(1)}, f32[4,2,512]{2,1,0:T(2,128)S(1)}, f32[4,2,512,128]{3,2,1,0:T(8,128)}, f32[4,2,512]{2,1,0:T(2,128)}, f32[4,2,...) conditional(s32[]{:T(128)} %convert_element_type.81, (bf16[2,2,512,4,128]{4,2,3,1,0:T(8,128)(2,1)S(1)}, ...), branch_computations={%region_5.7_spmd, %region_8.12_spmd} | conditional | flops 2183151616 | bytes 84377736 | solution.py:70
  393.9 8.7 %fusion.2 = f32[4,2,512]{2,1,0:T(2,128)S(1)} fusion(f32[4,1024,512,2]{2,1,3,0:T(8,128)} %get-tuple-element.414, f32[4,2,512]{2,1,0:T(2,128)} %max.6), kind=kLoop, calls=%fused_computation.4 | loop fusion | flops 12578816 | bytes 16809984 | tf_op jit(solution)/shard_map/while/body/eval_jaxpr/cond/branch_0_fun/reduce_sum | solution.py:19
  417.1 23.0 %collective-permute-done = bf16[2,2,512,4,128]{4,2,3,1,0:T(8,128)(2,1)S(1)} collective-permute-done((bf16[2,2,512,4,128]{4,2,3,1,0:T(8,128)(2,1)}, bf16[2,2,512,4,128]{4,2,3,1,0:T(8,128)(2,1)S(1)}, u32[]{:S(2)}, u32[]{:S(2)}) %collective-permute-start) | collective-permute-done | bytes 2097184 | tf_op jit(solution)/shard_map/while/body/eval_jaxpr/ppermute | solution.py:68
  440.1 27.6 %conditional.2 = (f32[4,2,512]{2,1,0:T(2,128)S(1)}, f32[4,2,512]{2,1,0:T(2,128)S(1)}, f32[4,2,512,128]{3,2,1,0:T(8,128)}, f32[4,2,512]{2,1,0:T(2,128)}, f32[4,2,...) conditional(s32[]{:T(128)} %convert_element_type.81, (bf16[2,2,512,4,128]{4,2,3,1,0:T(8,128)(2,1)S(1)}, ...), branch_computations={%region_5.7_spmd, %region_8.12_spmd} | conditional | flops 2183151616 | bytes 84377736 | solution.py:70
  449.0 8.7 %fusion.2 = f32[4,2,512]{2,1,0:T(2,128)S(1)} fusion(f32[4,1024,512,2]{2,1,3,0:T(8,128)} %get-tuple-element.414, f32[4,2,512]{2,1,0:T(2,128)} %max.6), kind=kLoop, calls=%fused_computation.4 | loop fusion | flops 12578816 | bytes 16809984 | tf_op jit(solution)/shard_map/while/body/eval_jaxpr/cond/branch_0_fun/reduce_sum | solution.py:19
  472.2 23.0 %collective-permute-done = bf16[2,2,512,4,128]{4,2,3,1,0:T(8,128)(2,1)S(1)} collective-permute-done((bf16[2,2,512,4,128]{4,2,3,1,0:T(8,128)(2,1)}, bf16[2,2,512,4,128]{4,2,3,1,0:T(8,128)(2,1)S(1)}, u32[]{:S(2)}, u32[]{:S(2)}) %collective-permute-start) | collective-permute-done | bytes 2097184 | tf_op jit(solution)/shard_map/while/body/eval_jaxpr/ppermute | solution.py:68
  495.2 27.6 %conditional.2 = (f32[4,2,512]{2,1,0:T(2,128)S(1)}, f32[4,2,512]{2,1,0:T(2,128)S(1)}, f32[4,2,512,128]{3,2,1,0:T(8,128)}, f32[4,2,512]{2,1,0:T(2,128)}, f32[4,2,...) conditional(s32[]{:T(128)} %convert_element_type.81, (bf16[2,2,512,4,128]{4,2,3,1,0:T(8,128)(2,1)S(1)}, ...), branch_computations={%region_5.7_spmd, %region_8.12_spmd} | conditional | flops 2183151616 | bytes 84377736 | solution.py:70
  504.0 8.7 %fusion.2 = f32[4,2,512]{2,1,0:T(2,128)S(1)} fusion(f32[4,1024,512,2]{2,1,3,0:T(8,128)} %get-tuple-element.414, f32[4,2,512]{2,1,0:T(2,128)} %max.6), kind=kLoop, calls=%fused_computation.4 | loop fusion | flops 12578816 | bytes 16809984 | tf_op jit(solution)/shard_map/while/body/eval_jaxpr/cond/branch_0_fun/reduce_sum | solution.py:19
  527.3 23.0 %collective-permute-done = bf16[2,2,512,4,128]{4,2,3,1,0:T(8,128)(2,1)S(1)} collective-permute-done((bf16[2,2,512,4,128]{4,2,3,1,0:T(8,128)(2,1)}, bf16[2,2,512,4,128]{4,2,3,1,0:T(8,128)(2,1)S(1)}, u32[]{:S(2)}, u32[]{:S(2)}) %collective-permute-start) | collective-permute-done | bytes 2097184 | tf_op jit(solution)/shard_map/while/body/eval_jaxpr/ppermute | solution.py:68
  550.2 27.6 %conditional.2 = (f32[4,2,512]{2,1,0:T(2,128)S(1)}, f32[4,2,512]{2,1,0:T(2,128)S(1)}, f32[4,2,512,128]{3,2,1,0:T(8,128)}, f32[4,2,512]{2,1,0:T(2,128)}, f32[4,2,...) conditional(s32[]{:T(128)} %convert_element_type.81, (bf16[2,2,512,4,128]{4,2,3,1,0:T(8,128)(2,1)S(1)}, ...), branch_computations={%region_5.7_spmd, %region_8.12_spmd} | conditional | flops 2183151616 | bytes 84377736 | solution.py:70
  550.4 8.1 bitcast_reduce_fusion
  559.1 8.7 %fusion.2 = f32[4,2,512]{2,1,0:T(2,128)S(1)} fusion(f32[4,1024,512,2]{2,1,3,0:T(8,128)} %get-tuple-element.414, f32[4,2,512]{2,1,0:T(2,128)} %max.6), kind=kLoop, calls=%fused_computation.4 | loop fusion | flops 12578816 | bytes 16809984 | tf_op jit(solution)/shard_map/while/body/eval_jaxpr/cond/branch_0_fun/reduce_sum | solution.py:19
  585.5 15.0 %convolution_bitcast_fusion = f32[1024,5376]{1,0:T(8,128)} fusion(bf16[1024,128,2,4]{1,0,3,2:T(8,128)(2,1)S(1)} %bitcast.181, bf16[4,2,128,5376]{3,2,1,0:T(8,128)(2,1)S(1)} %bitcast.191), kind=kOutput, calls=%fused_computation.50 | convolution fusion | flops 11274289152 | bytes 35127296 | tf_op jit(solution)/shard_map/hgsqe,hged->sqd/dot_general | solution.py:80
  600.5 208.4 %reduce-scatter.2.cloned.1.call-done = f32[256,5376]{1,0:T(8,128)} async-done(((f32[1024,5376]{1,0:T(8,128)}), f32[256,5376]{1,0:T(8,128)}) %reduce-scatter.2.cloned.1.call-update) | async-done | bytes 5505040 | tf_op jit(solution)/shard_map/reduce_scatter | solution.py:81
  (133 shorter events, 182.1 us)
Async XLA Ops:
  6.5 109.2 %all-gather.2.cloned.1.call-start = ((), (), s32[]{:S(2)}) async-start(), calls=%async_computation.1 | async-start | bytes 13762560 | tf_op jit(solution)/shard_map/all_gather | solution.py:32
  7.3 801.6 %reduce-scatter.2.cloned.1.call-start = ((), (), s32[]{:S(2)}) async-start(), calls=%async_computation.2 | async-start | bytes 27525120 | tf_op jit(solution)/shard_map/reduce_scatter | solution.py:81
  126.1 1.1 copy-start.10
  139.1 2.5 copy-start.6
  161.4 3.2 copy-start.5
  173.9 9.3 %copy-start.7 = (bf16[1,2,512,4,128]{2,1,4,3,0:T(2,128)(2,1)S(1)}, bf16[1,2,512,4,128]{2,1,4,3,0:T(2,128)(2,1)}, u32[]{:S(2)}) copy-start(bf16[1,2,512,4,128]{2,1,4,3,0:T(2,128)(2,1)} %stack_reshape.7) | copy-start | bytes 3145732
  188.9 7.6 copy-start.11
  196.4 9.6 %copy-start.8 = (bf16[1,2,512,4,128]{4,2,3,1,0:T(8,128)(2,1)S(1)}, bf16[1,2,512,4,128]{4,2,3,1,0:T(8,128)(2,1)}, u32[]{:S(2)}) copy-start(bf16[1,2,512,4,128]{4,2,3,1,0:T(8,128)(2,1)} %copy.19) | copy-start | bytes 3145732
  196.4 9.6 %copy-start.9 = (bf16[1,2,512,4,128]{4,2,3,1,0:T(8,128)(2,1)S(1)}, bf16[1,2,512,4,128]{4,2,3,1,0:T(8,128)(2,1)}, u32[]{:S(2)}) copy-start(bf16[1,2,512,4,128]{4,2,3,1,0:T(8,128)(2,1)} %copy.18) | copy-start | bytes 3145732
  207.8 25.0 %collective-permute-start = (bf16[2,2,512,4,128]{4,2,3,1,0:T(8,128)(2,1)}, bf16[2,2,512,4,128]{4,2,3,1,0:T(8,128)(2,1)S(1)}, u32[]{:S(2)}, u32[]{:S(2)}) collective-permute-start(bf16[2,2,512,4,128]{4,2,3,1,0:T(8,128)(2,1)} %get-tuple-element.552), channel_id=1, source_target_pairs={{0,1},{1,2},{2,3},{3,4},{4,5},{5,6},{6,7},{7,0},{8,9},{9,10},{10,1... | collective-permute-start | bytes 6291464 | tf_op jit(solution)/shard_map/while/body/eval_jaxpr/ppermute | solution.py:68
  232.8 4.0 copy-start.4
  239.5 5.5 copy-start.1
  248.6 1.3 copy-start.3
  251.9 25.5 %collective-permute-start = (bf16[2,2,512,4,128]{4,2,3,1,0:T(8,128)(2,1)}, bf16[2,2,512,4,128]{4,2,3,1,0:T(8,128)(2,1)S(1)}, u32[]{:S(2)}, u32[]{:S(2)}) collective-permute-start(bf16[2,2,512,4,128]{4,2,3,1,0:T(8,128)(2,1)} %get-tuple-element.552), channel_id=1, source_target_pairs={{0,1},{1,2},{2,3},{3,4},{4,5},{5,6},{6,7},{7,0},{8,9},{9,10},{10,1... | collective-permute-start | bytes 6291464 | tf_op jit(solution)/shard_map/while/body/eval_jaxpr/ppermute | solution.py:68
  286.3 9.4 %copy-start = (f32[4,2,512,128]{3,2,1,0:T(8,128)S(1)}, f32[4,2,512,128]{3,2,1,0:T(8,128)}, u32[]{:S(2)}) copy-start(f32[4,2,512,128]{3,2,1,0:T(8,128)} %get-tuple-element.328) | copy-start | bytes 6291460 | tf_op jit(solution)/shard_map/while/body/eval_jaxpr/cond
  303.6 1.3 copy-start.2
  307.0 23.0 %collective-permute-start = (bf16[2,2,512,4,128]{4,2,3,1,0:T(8,128)(2,1)}, bf16[2,2,512,4,128]{4,2,3,1,0:T(8,128)(2,1)S(1)}, u32[]{:S(2)}, u32[]{:S(2)}) collective-permute-start(bf16[2,2,512,4,128]{4,2,3,1,0:T(8,128)(2,1)} %get-tuple-element.552), channel_id=1, source_target_pairs={{0,1},{1,2},{2,3},{3,4},{4,5},{5,6},{6,7},{7,0},{8,9},{9,10},{10,1... | collective-permute-start | bytes 6291464 | tf_op jit(solution)/shard_map/while/body/eval_jaxpr/ppermute | solution.py:68
  338.8 9.4 %copy-start = (f32[4,2,512,128]{3,2,1,0:T(8,128)S(1)}, f32[4,2,512,128]{3,2,1,0:T(8,128)}, u32[]{:S(2)}) copy-start(f32[4,2,512,128]{3,2,1,0:T(8,128)} %get-tuple-element.328) | copy-start | bytes 6291460 | tf_op jit(solution)/shard_map/while/body/eval_jaxpr/cond
  356.2 1.3 copy-start.2
  359.6 25.5 %collective-permute-start = (bf16[2,2,512,4,128]{4,2,3,1,0:T(8,128)(2,1)}, bf16[2,2,512,4,128]{4,2,3,1,0:T(8,128)(2,1)S(1)}, u32[]{:S(2)}, u32[]{:S(2)}) collective-permute-start(bf16[2,2,512,4,128]{4,2,3,1,0:T(8,128)(2,1)} %get-tuple-element.552), channel_id=1, source_target_pairs={{0,1},{1,2},{2,3},{3,4},{4,5},{5,6},{6,7},{7,0},{8,9},{9,10},{10,1... | collective-permute-start | bytes 6291464 | tf_op jit(solution)/shard_map/while/body/eval_jaxpr/ppermute | solution.py:68
  393.9 9.4 %copy-start = (f32[4,2,512,128]{3,2,1,0:T(8,128)S(1)}, f32[4,2,512,128]{3,2,1,0:T(8,128)}, u32[]{:S(2)}) copy-start(f32[4,2,512,128]{3,2,1,0:T(8,128)} %get-tuple-element.328) | copy-start | bytes 6291460 | tf_op jit(solution)/shard_map/while/body/eval_jaxpr/cond
  411.3 1.3 copy-start.2
  414.6 25.5 %collective-permute-start = (bf16[2,2,512,4,128]{4,2,3,1,0:T(8,128)(2,1)}, bf16[2,2,512,4,128]{4,2,3,1,0:T(8,128)(2,1)S(1)}, u32[]{:S(2)}, u32[]{:S(2)}) collective-permute-start(bf16[2,2,512,4,128]{4,2,3,1,0:T(8,128)(2,1)} %get-tuple-element.552), channel_id=1, source_target_pairs={{0,1},{1,2},{2,3},{3,4},{4,5},{5,6},{6,7},{7,0},{8,9},{9,10},{10,1... | collective-permute-start | bytes 6291464 | tf_op jit(solution)/shard_map/while/body/eval_jaxpr/ppermute | solution.py:68
  449.0 9.4 %copy-start = (f32[4,2,512,128]{3,2,1,0:T(8,128)S(1)}, f32[4,2,512,128]{3,2,1,0:T(8,128)}, u32[]{:S(2)}) copy-start(f32[4,2,512,128]{3,2,1,0:T(8,128)} %get-tuple-element.328) | copy-start | bytes 6291460 | tf_op jit(solution)/shard_map/while/body/eval_jaxpr/cond
  466.3 1.3 copy-start.2
  469.7 25.5 %collective-permute-start = (bf16[2,2,512,4,128]{4,2,3,1,0:T(8,128)(2,1)}, bf16[2,2,512,4,128]{4,2,3,1,0:T(8,128)(2,1)S(1)}, u32[]{:S(2)}, u32[]{:S(2)}) collective-permute-start(bf16[2,2,512,4,128]{4,2,3,1,0:T(8,128)(2,1)} %get-tuple-element.552), channel_id=1, source_target_pairs={{0,1},{1,2},{2,3},{3,4},{4,5},{5,6},{6,7},{7,0},{8,9},{9,10},{10,1... | collective-permute-start | bytes 6291464 | tf_op jit(solution)/shard_map/while/body/eval_jaxpr/ppermute | solution.py:68
  504.0 9.4 %copy-start = (f32[4,2,512,128]{3,2,1,0:T(8,128)S(1)}, f32[4,2,512,128]{3,2,1,0:T(8,128)}, u32[]{:S(2)}) copy-start(f32[4,2,512,128]{3,2,1,0:T(8,128)} %get-tuple-element.328) | copy-start | bytes 6291460 | tf_op jit(solution)/shard_map/while/body/eval_jaxpr/cond
  521.4 1.3 copy-start.2
  524.8 25.5 %collective-permute-start = (bf16[2,2,512,4,128]{4,2,3,1,0:T(8,128)(2,1)}, bf16[2,2,512,4,128]{4,2,3,1,0:T(8,128)(2,1)S(1)}, u32[]{:S(2)}, u32[]{:S(2)}) collective-permute-start(bf16[2,2,512,4,128]{4,2,3,1,0:T(8,128)(2,1)} %get-tuple-element.552), channel_id=1, source_target_pairs={{0,1},{1,2},{2,3},{3,4},{4,5},{5,6},{6,7},{7,0},{8,9},{9,10},{10,1... | collective-permute-start | bytes 6291464 | tf_op jit(solution)/shard_map/while/body/eval_jaxpr/ppermute | solution.py:68
  559.1 9.4 %copy-start = (f32[4,2,512,128]{3,2,1,0:T(8,128)S(1)}, f32[4,2,512,128]{3,2,1,0:T(8,128)}, u32[]{:S(2)}) copy-start(f32[4,2,512,128]{3,2,1,0:T(8,128)} %get-tuple-element.328) | copy-start | bytes 6291460 | tf_op jit(solution)/shard_map/while/body/eval_jaxpr/cond
  576.5 1.3 copy-start.2
  580.1 5.4 copy-start.12
Sparse Core Ops, SparseCore 0:
  8.9 106.7 all-gather.1
  600.6 208.2 reduce-scatter.1
where the time goes:
time: 837 us; the launch traced here: 821 us
  waiting for transfers between devices  478 us (57%)
  matrix products  186 us (22%)
  other arithmetic  87.2 us (10%)
  local copies, waits for them, and re-layouts  39.8 us (5%)
  starting transfers between devices  14.6 us (2%)
  between operations  14.1 us (2%)
    reduce_scatter x1, waiting for transfers between devices, local_layer(): y_loc = lax.psum_scatter(partial, 'tp', scatter_dimension=0, tiled=True)  208 us
    ppermute x7, waiting for transfers between devices, kv_step(): kv_held = lax.ppermute(kv_held, 'cp', shift_pairs)  161 us
    all_gather x1, waiting for transfers between devices, local_layer(): x_block = lax.all_gather(x_loc, 'tp', axis=0, tiled=True)  108 us
    dot_general x10, matrix products, merge_block(): jnp.einsum('hgqk,khe->hgqe', p_block.astype(jnp.bfloat16), v_part, prefer...  73.1 us
    reduce_sum x10, other arithmetic, merge_block(): new_sum = run_sum * rescale + p_block.sum(axis=-1)  66.5 us
    dot_general x10, matrix products, block_scores(): jnp.einsum('qhge,khe->hgqk', q_part, k_part, preferred_element_type=jnp.f...  62.2 us
  transfers between devices with their start and end apart: 9, of which 9 were waited for; matrix products, arithmetic and copies ran while one was open for 0% of the time, Pallas kernels for 0%

commit v1 on v0

v1 whole, which is shorter than its diff:
```python
import functools
import math

import jax
import jax.numpy as jnp
from jax import lax
from jax.experimental import pallas as pl
from jax.experimental.pallas import tpu as pltpu
from jax.sharding import PartitionSpec as P

HEAD_DIM = 128
F32 = jnp.float32
BF16 = jnp.bfloat16
MESH = pl.DeviceIdType.MESH
SCALE_LOG2 = math.log2(math.e) / math.sqrt(float(HEAD_DIM))
N_TILE = 512
VMEM_LIMIT = 62 * 1024 * 1024


def gather_project_kernel(cp_size, x_ref, wq_ref, wk_ref, wv_ref, q_out, kv_out,
                          x_buf, w_buf, out_buf, load_sem, x_send, x_recv, kv_send, kv_recv, store_sem):
    tp_rank = lax.axis_index("tp")
    cp_rank = lax.axis_index("cp")
    n_tp = 4
    x_rank, core = cp_rank // 2, lax.rem(cp_rank, 2)
    n_x = cp_size // 2
    up_tp, down_tp = lax.rem(tp_rank + 1, n_tp), lax.rem(tp_rank + n_tp - 1, n_tp)
    opp_tp = lax.rem(tp_rank + 2, n_tp)
    up_x, down_x = lax.rem(x_rank + 1, n_x), lax.rem(x_rank + n_x - 1, n_x)
    opp_x = lax.rem(x_rank + 2, n_x)
    up_cp, down_cp, opp_cp = up_x * 2 + core, down_x * 2 + core, opp_x * 2 + core
    partner = x_rank * 2 + 1 - core
    rows = x_ref.shape[0]
    half = rows // 2
    piece = 2 * rows
    n_cols = wk_ref.shape[1]

    loads = [pltpu.make_async_copy(x_ref, x_buf.at[0], load_sem.at[0])]
    w_parts = [(wk_ref, 0), (wv_ref, 0), (wq_ref, 0), (wq_ref, N_TILE)]
    for idx, (ref, col) in enumerate(w_parts):
        loads.append(pltpu.make_async_copy(ref.at[:, pl.ds(col, N_TILE)], w_buf.at[idx], load_sem.at[1 + idx]))
    for copy in loads:
        copy.start()

    barrier = pltpu.get_barrier_semaphore()
    for target in ({"tp": up_tp}, {"tp": down_tp}, {"cp": up_cp}, {"cp": down_cp}, {"cp": partner}):
        pl.semaphore_signal(barrier, inc=1, device_id=target, device_id_type=MESH)
    pl.semaphore_wait(barrier, 5)

    def x_copy(src, stage, part, idx, target):
        return pltpu.make_async_remote_copy(
            src_ref=src, dst_ref=x_buf.at[stage, pl.ds(part * half, half), :],
            send_sem=x_send.at[idx], recv_sem=x_recv.at[idx], device_id={"tp": target}, device_id_type=MESH)

    first, second = x_ref.at[pl.ds(0, half), :], x_ref.at[pl.ds(half, half), :]
    x_copies = [
        x_copy(first, 1, 0, 0, up_tp),
        x_copy(second, 2, 0, 1, up_tp),
        x_copy(second, 1, 1, 2, down_tp),
        x_copy(first, 2, 1, 3, down_tp),
        x_copy(x_buf.at[1, pl.ds(0, half), :], 3, 0, 4, up_tp),
        x_copy(x_buf.at[1, pl.ds(half, half), :], 3, 1, 5, down_tp),
    ]
    x_copies[0].start()
    x_copies[2].start()
    x_copies[1].start()
    x_copies[3].start()

    owners = [
        ((tp_rank, 0), (tp_rank, 1)),
        ((down_tp, 0), (up_tp, 1)),
        ((down_tp, 1), (up_tp, 0)),
        ((opp_tp, 0), (opp_tp, 1)),
    ]

    def kv_rows(cp_owner, stage, part):
        tp_owner, which = owners[stage][part]
        index = jnp.where(tp_owner < 2, cp_owner, 2 * cp_size - 1 - cp_owner)
        row = index * piece + lax.rem(tp_owner, 2) * rows + which * half
        return kv_out.at[pl.ds(pl.multiple_of(row, half), half), :]

    def kv_copy(src, dst, stage, idx, target):
        return pltpu.make_async_remote_copy(
            src_ref=src, dst_ref=dst, send_sem=kv_send.at[stage, idx], recv_sem=kv_recv.at[stage, idx],
            device_id={"cp": target}, device_id_type=MESH)

    def own_kv(stage, part):
        return out_buf.at[stage, pl.ds(part * half, half), pl.ds(0, 2 * n_cols)]

    def kv_sends(stage):
        copies = []
        for part in range(2):
            dst = kv_rows(cp_rank, stage, part)
            copies.append(kv_copy(own_kv(stage, part), dst, stage, part, up_cp))
            copies.append(kv_copy(own_kv(stage, part), dst, stage, 2 + part, down_cp))
            copies.append(kv_copy(own_kv(stage, part), dst, stage, 4 + part, partner))
        return copies

    def kv_forwards(stage):
        below = [kv_rows(down_cp, stage, part) for part in range(2)]
        above = [kv_rows(up_cp, stage, part) for part in range(2)]
        return [
            kv_copy(below[0], below[0], stage, 6, up_cp),
            kv_copy(above[1], above[1], stage, 7, down_cp),
            kv_copy(below[0], below[0], stage, 8, partner),
            kv_copy(above[1], above[1], stage, 9, partner),
            kv_copy(below[1], below[1], stage, 10, partner),
            kv_copy(above[0], above[0], stage, 11, partner),
        ]

    def kv_relays(stage):
        far = [kv_rows(opp_cp, stage, part) for part in range(2)]
        return [kv_copy(far[part], far[part], stage, 12 + part, partner) for part in range(2)]

    stores = []

    def project(stage):
        def tile(idx, carry):
            val = jnp.dot(x_buf[stage], w_buf[idx], preferred_element_type=F32)
            out_buf[stage, :, pl.ds(pl.multiple_of(idx * N_TILE, N_TILE), N_TILE)] = val.astype(BF16)
            return carry

        if stage == 0:
            for idx in range(4):
                loads[1 + idx].wait()
        lax.fori_loop(0, 4, tile, 0)
        for part in range(2):
            tp_owner, which = owners[stage][part]
            row = pl.multiple_of(tp_owner * rows + which * half, half)
            q_store = pltpu.make_async_copy(
                out_buf.at[stage, pl.ds(part * half, half), pl.ds(2 * n_cols, q_out.shape[1])],
                q_out.at[pl.ds(row, half), :], store_sem.at[stage, part])
            kv_store = pltpu.make_async_copy(own_kv(stage, part), kv_rows(cp_rank, stage, part),
                                             store_sem.at[stage, 2 + part])
            for copy in (q_store, kv_store):
                copy.start()
                stores.append(copy)

    sent = []
    for stage in range(4):
        if stage == 0:
            loads[0].wait()
        elif stage == 1:
            x_copies[0].wait_recv()
            x_copies[4].start()
            x_copies[2].wait_recv()
            x_copies[5].start()
        elif stage == 2:
            x_copies[1].wait_recv()
            x_copies[3].wait_recv()
        else:
            x_copies[4].wait_recv()
            x_copies[5].wait_recv()
        project(stage)
        sends = kv_sends(stage)
        for copy in sends:
            copy.start()
        if stage > 0:
            for copy in forwards[:2]:
                copy.wait_recv()
            relays = kv_relays(stage - 1)
            for copy in relays:
                copy.start()
            sent += relays
        forwards = kv_forwards(stage)
        by_idx = {0: sends[0], 2: sends[1], 1: sends[3], 3: sends[4]}
        by_idx[0].wait_recv()
        forwards[0].start()
        by_idx[3].wait_recv()
        forwards[1].start()
        forwards[2].start()
        forwards[3].start()
        by_idx[1].wait_recv()
        forwards[4].start()
        by_idx[2].wait_recv()
        forwards[5].start()
        sent += sends + forwards
    for copy in forwards[:2]:
        copy.wait_recv()
    relays = kv_relays(3)
    for copy in relays:
        copy.start()
    sent += relays
    for stage in range(4):
        arrivals = kv_sends(stage)
        arrivals = [arrivals[2], arrivals[5]] + kv_forwards(stage)[2:] + kv_relays(stage)
        for copy in arrivals:
            copy.wait_recv()
    for copy in sent + x_copies:
        copy.wait_send()
    for copy in stores:
        copy.wait()


def gather_project(x_loc, w_q, w_k, w_v, cp_size):
    rows, width = x_loc.shape
    q_cols, k_cols = w_q.shape[1], w_k.shape[1]
    any_spec = pl.BlockSpec(memory_space=pl.ANY)
    return pl.pallas_call(
        functools.partial(gather_project_kernel, cp_size),
        out_shape=(jax.ShapeDtypeStruct((4 * rows, q_cols), BF16),
                   jax.ShapeDtypeStruct((4 * rows * cp_size, 2 * k_cols), BF16)),
        in_specs=[any_spec] * 4,
        out_specs=(any_spec, any_spec),
        scratch_shapes=[
            pltpu.VMEM((4, rows, width), BF16),
            pltpu.VMEM((4, width, N_TILE), BF16),
            pltpu.VMEM((4, rows, q_cols + 2 * k_cols), BF16),
            pltpu.SemaphoreType.DMA((5,)),
            pltpu.SemaphoreType.DMA((6,)),
            pltpu.SemaphoreType.DMA((6,)),
            pltpu.SemaphoreType.DMA((4, 14)),
            pltpu.SemaphoreType.DMA((4, 14)),
            pltpu.SemaphoreType.DMA((4, 4)),
        ],
        compiler_params=pltpu.CompilerParams(collective_id=0, has_side_effects=True, vmem_limit_bytes=VMEM_LIMIT),
        cost_estimate=pl.CostEstimate(flops=2 * 4 * rows * width * (q_cols + 2 * k_cols), bytes_accessed=80_000_000, transcendentals=0),
        name="gather_project",
    )(x_loc, w_q, w_k, w_v)


def attention_kernel(n_pieces, group, q_chunk, q_ref, k_ref, v_ref, o_ref, acc, run_max, run_sum):
    rank = lax.axis_index("cp")
    piece = q_ref.shape[0] // 2

    def block(which, first, key_row):
        keys = k_ref[pl.ds(key_row, piece), :]
        vals = v_ref[pl.ds(key_row, piece), :]
        chains = [(g, c) for g in range(group) for c in range(piece // q_chunk)]
        scores = []
        for g, c in chains:
            q = q_ref[pl.ds(which * piece + c * q_chunk, q_chunk), g * HEAD_DIM:(g + 1) * HEAD_DIM]
            scores.append(lax.dot_general(q, keys, (((1,), (1,)), ((), ())), preferred_element_type=F32))
        for (g, c), s in zip(chains, scores):
            if first:
                key_pos = lax.broadcasted_iota(jnp.int32, s.shape, 1)
                q_pos = lax.broadcasted_iota(jnp.int32, s.shape, 0) + c * q_chunk
                s = jnp.where(key_pos <= q_pos, s, -jnp.inf)
            sl = slice(c * q_chunk, (c + 1) * q_chunk)
            block_max = jnp.broadcast_to(jnp.max(s, axis=1, keepdims=True) * SCALE_LOG2, (q_chunk, HEAD_DIM))
            if first:
                new_max = block_max
            else:
                old_max = run_max[g, sl, :]
                new_max = jnp.maximum(old_max, block_max)
            p = jnp.exp2(s * SCALE_LOG2 - jnp.concatenate([new_max] * (piece // HEAD_DIM), axis=1))
            sums = p[:, :HEAD_DIM]
            for t in range(1, piece // HEAD_DIM):
                sums = sums + p[:, t * HEAD_DIM:(t + 1) * HEAD_DIM]
            weighted = jnp.dot(p.astype(BF16), vals, preferred_element_type=F32)
            if first:
                run_sum[g, sl, :] = sums
                acc[g, sl, :] = weighted
            else:
                rescale = jnp.exp2(old_max - new_max)
                run_sum[g, sl, :] = run_sum[g, sl, :] * rescale + sums
                acc[g, sl, :] = acc[g, sl, :] * rescale + weighted
            run_max[g, sl, :] = new_max

    for which in range(2):
        index = rank if which == 0 else n_pieces - 1 - rank
        block(which, True, pl.multiple_of(index * piece, piece))

        def body(j, carry):
            block(which, False, pl.multiple_of(j * piece, piece))
            return carry

        lax.fori_loop(0, index, body, 0)
        for g in range(group):
            total = jnp.sum(run_sum[g], axis=1, keepdims=True)
            o_ref[pl.ds(which * piece, piece), g * HEAD_DIM:(g + 1) * HEAD_DIM] = (acc[g] / total).astype(BF16)


def attention(q, kv):
    rows = q.shape[0]
    piece = rows // 2
    kv_heads = kv.shape[1] // (2 * HEAD_DIM)
    group = q.shape[1] // HEAD_DIM // kv_heads
    n_pieces = kv.shape[0] // piece
    return pl.pallas_call(
        functools.partial(attention_kernel, n_pieces, group, piece),
        grid=(kv_heads,),
        in_specs=[pl.BlockSpec((rows, group * HEAD_DIM), lambda h: (0, h)),
                  pl.BlockSpec((kv.shape[0], HEAD_DIM), lambda h: (0, h)),
                  pl.BlockSpec((kv.shape[0], HEAD_DIM), lambda h: (0, kv_heads + h))],
        out_specs=pl.BlockSpec((rows, group * HEAD_DIM), lambda h: (0, h)),
        out_shape=jax.ShapeDtypeStruct(q.shape, BF16),
        scratch_shapes=[pltpu.VMEM((group, piece, HEAD_DIM), F32)] * 3,
        compiler_params=pltpu.CompilerParams(vmem_limit_bytes=48 * 1024 * 1024),
        cost_estimate=pl.CostEstimate(flops=40_000_000_000, bytes_accessed=22_000_000, transcendentals=36_000_000),
        name="attention",
    )(q, kv, kv)


def solution(mesh):
    cp_size = mesh.shape["cp"]
    row_spec = P(("dp", "cp", "tp"), None)

    def local_layer(x_loc, w_q, w_k, w_v, w_o):
        q, kv = gather_project(x_loc, w_q, w_k, w_v, cp_size)
        share = w_o.shape[0] // cp_size
        w_slice = lax.dynamic_slice_in_dim(w_o, lax.axis_index("cp") * share, share, axis=0)
        w_slice, kv = lax.optimization_barrier((w_slice, kv))
        w_full = lax.all_gather(w_slice, ("tp", "cp"), axis=0, tiled=True)
        attn = attention(q, kv)
        attn_rows = lax.all_to_all(attn, "tp", split_axis=0, concat_axis=1, tiled=True)
        return jnp.dot(attn_rows, w_full, preferred_element_type=F32).astype(BF16)

    return jax.shard_map(local_layer, mesh=mesh, in_specs=(row_spec, P(None, "tp"), P(None, "tp"), P(None, "tp"), P("tp", None)), out_specs=row_spec, check_vma=False)
```

time: 837 us -> 319 us (0.38); the launches traced: 821 us -> 319 us
  waiting for transfers between devices: 478 us -> 36.9 us
  Pallas kernels: 0 us -> 190 us
  matrix products: 186 us -> 19.6 us
  other arithmetic: 87.2 us -> 0 us
  blocking collectives: 0 us -> 52.6 us
  local copies, waits for them, and re-layouts: 39.8 us -> 6.68 us
  starting transfers between devices: 14.6 us -> 0.01 us
    reduce_scatter x1 -> x0, waiting for transfers between devices: 208 us -> none  [local_layer(): y_loc = lax.psum_scatter(partial, 'tp', scatter_dimension=0, tiled=True)]
    pallas_call x0 -> x2, Pallas kernels: none -> 190 us  [the longest x1 125 us: gather_project(): pl.pallas_call(functools.partial(gather_project_kernel, cp_size), out_sha...]
    dot_general x24 -> x1, matrix products: 186 us -> 19.6 us  [local_layer(): return jnp.dot(attn_rows, w_full, preferred_element_type=F32).astype(BF16)]
    ppermute x7 -> x0, waiting for transfers between devices: 161 us -> none  [kv_step(): kv_held = lax.ppermute(kv_held, 'cp', shift_pairs)]
    all_gather x1, waiting for transfers between devices: 108 us -> 36.8 us  [local_layer(): w_full = lax.all_gather(w_slice, ('tp', 'cp'), axis=0, tiled=True)]
    reduce_sum x10 -> x0, other arithmetic: 66.5 us -> none  [merge_block(): new_sum = run_sum * rescale + p_block.sum(axis=-1)]
    all_to_all x0 -> x1, blocking collectives: none -> 52.6 us  [local_layer(): lax.all_to_all(attn, 'tp', split_axis=0, concat_axis=1, tiled=True)]
    while x16 -> x0, local copies, waits for them, and re-layouts: 16.5 us -> none
  transfers between devices with their start and end apart: 9 -> 1, of which waited for: 9 -> 1; matrix products, arithmetic and copies ran while one was open for 0% -> 1% of each run, Pallas kernels for 0% -> 20%
where the time goes in v1:
time: 319 us
  Pallas kernels  190 us (60%)
  blocking collectives  52.6 us (16%)
  waiting for transfers between devices  36.9 us (12%)
  matrix products  19.6 us (6%)
  between operations  13.4 us (4%)
  local copies, waits for them, and re-layouts  6.68 us (2%)
    pallas_call x1, Pallas kernels, gather_project(): pl.pallas_call(functools.partial(gather_project_kernel, cp_size), out_sha...  125 us
    pallas_call x1, Pallas kernels, attention(): pl.pallas_call(functools.partial(attention_kernel, n_pieces, group, piece...  64.5 us
    all_to_all x1, blocking collectives, local_layer(): lax.all_to_all(attn, 'tp', split_axis=0, concat_axis=1, tiled=True)  52.6 us
    all_gather x1, waiting for transfers between devices, local_layer(): w_full = lax.all_gather(w_slice, ('tp', 'cp'), axis=0, tiled=True)  36.8 us
    dot_general x1, matrix products, local_layer(): return jnp.dot(attn_rows, w_full, preferred_element_type=F32).astype(BF16)  19.6 us
  transfers between devices with their start and end apart: 1, of which 1 were waited for; matrix products, arithmetic and copies ran while one was open for 1% of the time, Pallas kernels for 20%

profile of v1, /device:TPU:97, one launch (start us, length us, event | category | flops | bytes accessed | tf_op | source)
XLA Modules:
  0.0 318.8 jit_solution(15845597189385426965)
XLA Ops:
  6.5 0.0 all-gather.2.cloned.1.call-start
  6.6 2.5 constant_dynamic-slice_fusion
  9.1 125.1 %gather_project.1 = (bf16[1024,1024]{1,0:T(8,128)(2,1)}, bf16[8192,1024]{1,0:T(8,128)(2,1)}) custom-call(bf16[256,5376]{1,0:T(8,128)(2,1)} %x_ref.1, bf16[5376,1024]{1,0:T(8,128)(2,1)} %wq_ref.1, bf16[5376,512]{1,0:T(8,128)(2,1)} %wk_ref.1, bf16[5376,512]{1,0:T(8,128)(2,1)} %wv_ref.1), custom_call_target="tpu_custom_call" | custom-call | flops 22548578304 | bytes 80000000 | tf_op jit(solution)/shard_map/gather_project/pallas_call | solution.py:199
  134.2 0.1 all-gather.2.cloned.1.call-update
  134.3 0.0 copy-start
  134.3 1.6 copy-done
  135.9 64.5 %attention.1 = bf16[1024,1024]{1,0:T(8,128)(2,1)S(1)} custom-call(bf16[1024,1024]{1,0:T(8,128)(2,1)S(1)} %copy-done, bf16[8192,1024]{1,0:T(8,128)(2,1)} %get-tuple-element.11.k_ref.v_ref, bf16[8192,1024]{1,0:T(8,128)(2,1)} %get-tuple-element.11.k_ref.v_ref), custom_call_target="tpu_custom_call" | custom-call | flops 40000000000 | bytes 22000000 | tf_op jit(solution)/shard_map/attention/pallas_call | solution.py:280
  200.4 2.6 copy.6
  203.0 52.6 %all_to_all.19 = bf16[4,256,1024]{1,2,0:T(8,128)(2,1)S(1)} all-to-all(bf16[4,256,1024]{1,2,0:T(8,128)(2,1)} %copy.6), channel_id=1, replica_groups=mesh['dp'=1,'tp'=4,'cp'=8] {'tp'}, dimensions={0} | all-to-all | bytes 4194304 | tf_op jit(solution)/shard_map/all_to_all | solution.py:306
  255.6 36.8 %all-gather.2.cloned.1.call-done = bf16[4096,5376]{1,0:T(8,128)(2,1)} async-done(((bf16[128,5376]{1,0:T(8,128)(2,1)}), bf16[4096,5376]{1,0:T(8,128)(2,1)}) %all-gather.2.cloned.1.call-update) | async-done | bytes 44040208 | tf_op jit(solution)/shard_map/all_gather | solution.py:304
  292.4 19.6 %convolution_convert_fusion = bf16[256,5376]{1,0:T(8,128)(2,1)} fusion(bf16[256,4096]{0,1:T(8,128)(2,1)S(1)} %bitcast.7, bf16[4096,5376]{1,0:T(8,128)(2,1)} %all-gather.2.cloned.1.call-done), kind=kOutput, calls=%fused_computation | convolution fusion | flops 11275665408 | bytes 48889856 | tf_op jit(solution)/shard_map/dot_general | solution.py:307
Async XLA Ops:
  6.5 285.8 %all-gather.2.cloned.1.call-start = ((), (), s32[]{:S(2)}) async-start(), calls=%async_computation.1 | async-start | bytes 45416448 | tf_op jit(solution)/shard_map/all_gather | solution.py:304
  134.3 1.6 copy-start
Sparse Core Ops, SparseCore 0:
  134.4 157.8 all-gather.1

commit v2 on v1

--- a/solution.py
+++ b/solution.py
@@ -17,8 +17,22 @@
 VMEM_LIMIT = 62 * 1024 * 1024
 
 
-def gather_project_kernel(cp_size, x_ref, wq_ref, wk_ref, wv_ref, q_out, kv_out,
-                          x_buf, w_buf, out_buf, load_sem, x_send, x_recv, kv_send, kv_recv, store_sem):
+def wo_window(parity, which, core, rows, cols):
+    row = pl.multiple_of(parity * (rows // 2) + which * (rows // 4), rows // 4)
+    col = pl.multiple_of(core * (cols // 2), HEAD_DIM)
+    return pl.ds(row, rows // 4), pl.ds(col, cols // 2)
+
+
+def tp_block_copy(wo_ref, wo_out, rel, which, target, send_sem, recv_sem):
+    cp_rank = lax.axis_index("cp")
+    window = wo_window(lax.rem(cp_rank // 2, 2), which, lax.rem(cp_rank, 2), *wo_ref.shape)
+    return pltpu.make_async_remote_copy(
+        src_ref=wo_ref.at[window], dst_ref=wo_out.at[(rel,) + window], send_sem=send_sem, recv_sem=recv_sem,
+        device_id={"tp": target}, device_id_type=MESH)
+
+
+def gather_project_kernel(cp_size, x_ref, wq_ref, wk_ref, wv_ref, wo_ref, q_out, kv_out, wo_out,
+                          x_buf, w_buf, out_buf, load_sem, x_send, x_recv, kv_send, kv_recv, store_sem, wo_send, wo_recv):
     tp_rank = lax.axis_index("tp")
     cp_rank = lax.axis_index("cp")
     n_tp = 4
@@ -151,6 +165,12 @@
         else:
             x_copies[4].wait_recv()
             x_copies[5].wait_recv()
+            wo_copies = [
+                tp_block_copy(wo_ref, wo_out, 0, 0, up_tp, wo_send.at[0], wo_recv.at[0]),
+                tp_block_copy(wo_ref, wo_out, 1, 1, down_tp, wo_send.at[1], wo_recv.at[1]),
+            ]
+            for copy in wo_copies:
+                copy.start()
         project(stage)
         sends = kv_sends(stage)
         for copy in sends:
@@ -186,22 +206,25 @@
         arrivals = [arrivals[2], arrivals[5]] + kv_forwards(stage)[2:] + kv_relays(stage)
         for copy in arrivals:
             copy.wait_recv()
-    for copy in sent + x_copies:
+    for copy in wo_copies:
+        copy.wait_recv()
+    for copy in sent + x_copies + wo_copies:
         copy.wait_send()
     for copy in stores:
         copy.wait()
 
 
-def gather_project(x_loc, w_q, w_k, w_v, cp_size):
+def gather_project(x_loc, w_q, w_k, w_v, w_o, cp_size):
     rows, width = x_loc.shape
     q_cols, k_cols = w_q.shape[1], w_k.shape[1]
     any_spec = pl.BlockSpec(memory_space=pl.ANY)
     return pl.pallas_call(
         functools.partial(gather_project_kernel, cp_size),
         out_shape=(jax.ShapeDtypeStruct((4 * rows, q_cols), BF16),
-                   jax.ShapeDtypeStruct((4 * rows * cp_size, 2 * k_cols), BF16)),
-        in_specs=[any_spec] * 4,
-        out_specs=(any_spec, any_spec),
+                   jax.ShapeDtypeStruct((4 * rows * cp_size, 2 * k_cols), BF16),
+                   jax.ShapeDtypeStruct((3,) + w_o.shape, BF16)),
+        in_specs=[any_spec] * 5,
+        out_specs=(any_spec, any_spec, any_spec),
         scratch_shapes=[
             pltpu.VMEM((4, rows, width), BF16),
             pltpu.VMEM((4, width, N_TILE), BF16),
@@ -212,16 +235,113 @@
             pltpu.SemaphoreType.DMA((4, 14)),
             pltpu.SemaphoreType.DMA((4, 14)),
             pltpu.SemaphoreType.DMA((4, 4)),
+            pltpu.SemaphoreType.DMA((2,)),
+            pltpu.SemaphoreType.DMA((2,)),
         ],
         compiler_params=pltpu.CompilerParams(collective_id=0, has_side_effects=True, vmem_limit_bytes=VMEM_LIMIT),
         cost_estimate=pl.CostEstimate(flops=2 * 4 * rows * width * (q_cols + 2 * k_cols), bytes_accessed=80_000_000, transcendentals=0),
         name="gather_project",
-    )(x_loc, w_q, w_k, w_v)
-
-
-def attention_kernel(n_pieces, group, q_chunk, q_ref, k_ref, v_ref, o_ref, acc, run_max, run_sum):
-    rank = lax.axis_index("cp")
+    )(x_loc, w_q, w_k, w_v, w_o)
+
+
+def attention_kernel(n_pieces, group, q_chunk, cp_size, q_ref, k_ref, v_ref, wo_ref, wo_in, own_out, far_out, wo_out,
+                     acc, run_max, run_sum, o_buf, y_send, y_recv, x_send, x_recv, d_send, d_recv, o_send, o_recv, o_local):
+    del wo_in
+    head = pl.program_id(0)
+    n_heads = o_buf.shape[0]
+    tp_rank, rank = lax.axis_index("tp"), lax.axis_index("cp")
+    x_rank, core = rank // 2, lax.rem(rank, 2)
+    n_x = cp_size // 2
+    parity = lax.rem(x_rank, 2)
+    up_tp, down_tp, opp_tp = (lax.rem(tp_rank + d, 4) for d in (1, 3, 2))
+    up_cp = lax.rem(x_rank + 1, n_x) * 2 + core
+    down_cp = lax.rem(x_rank + n_x - 1, n_x) * 2 + core
+    partner = x_rank * 2 + 1 - core
     piece = q_ref.shape[0] // 2
+    rows = q_ref.shape[0] // 4
+    width = q_ref.shape[1]
+
+    def wo_block(rel, which, from_cp):
+        side = 1 - parity if from_cp else parity
+        return wo_out.at[(rel,) + wo_window(side, which, core, *wo_ref.shape)]
+
+    def forward(which):
+        return pltpu.make_async_remote_copy(
+            src_ref=wo_block(which, which, False), dst_ref=wo_block(2, which, False),
+            send_sem=y_send.at[which], recv_sem=y_recv.at[which],
+            device_id={"tp": up_tp if which == 0 else down_tp}, device_id_type=MESH)
+
+    def second(rel):
+        return tp_block_copy(wo_ref, wo_out, rel, 1 - rel, up_tp if rel == 0 else down_tp,
+                             y_send.at[2 + rel], y_recv.at[2 + rel])
+
+    def across(rel, which):
+        block = wo_block(rel, which, False)
+        return pltpu.make_async_remote_copy(
+            src_ref=block, dst_ref=block, send_sem=x_send.at[rel, which], recv_sem=x_recv.at[rel, which],
+            device_id={"cp": up_cp if which == 0 else down_cp}, device_id_type=MESH)
+
+    def relay(rel, which, from_cp):
+        block = wo_block(rel, which, from_cp)
+        slot = int(from_cp)
+        return pltpu.make_async_remote_copy(
+            src_ref=block, dst_ref=block, send_sem=d_send.at[slot, rel, which], recv_sem=d_recv.at[slot, rel, which],
+            device_id={"cp": partner}, device_id_type=MESH)
+
+    def result_copies(h):
+        copies = []
+        for rel, target in ((0, up_tp), (1, down_tp), (2, opp_tp)):
+            copies.append(pltpu.make_async_remote_copy(
+                src_ref=o_buf.at[h, pl.ds(pl.multiple_of(target * rows, rows), rows), :],
+                dst_ref=far_out.at[rel, :, pl.ds(h * width, width)],
+                send_sem=o_send.at[h, rel], recv_sem=o_recv.at[h, rel],
+                device_id={"tp": target}, device_id_type=MESH))
+        local = pltpu.make_async_copy(o_buf.at[h, pl.ds(pl.multiple_of(tp_rank * rows, rows), rows), :],
+                                      own_out.at[:, pl.ds(h * width, width)], o_local.at[h])
+        return copies, local
+
+    def send_result(h):
+        copies, local = result_copies(h)
+        for copy in copies + [local]:
+            copy.start()
+
+    def pass_on(rel, which):
+        across(rel, which).start()
+        relay(rel, which, False).start()
+
+    def relay_across(rel, which):
+        across(rel, which).wait_recv()
+        relay(rel, which, True).start()
+
+    @pl.when(head == 0)
+    def _():
+        barrier = pltpu.get_barrier_semaphore()
+        for target in ({"tp": up_tp}, {"tp": down_tp}, {"tp": opp_tp}, {"cp": up_cp}, {"cp": down_cp}, {"cp": partner}):
+            pl.semaphore_signal(barrier, inc=1, device_id=target, device_id_type=MESH)
+        pl.semaphore_wait(barrier, 6)
+        forward(0).start()
+        forward(1).start()
+        second(0).start()
+        second(1).start()
+        pass_on(0, 0)
+        pass_on(1, 1)
+
+    @pl.when(head == 1)
+    def _():
+        send_result(0)
+
+    @pl.when(head == 2)
+    def _():
+        for which in range(2):
+            forward(which).wait_recv()
+            pass_on(2, which)
+        relay_across(0, 0)
+        relay_across(1, 1)
+        send_result(1)
+
+    @pl.when(head == 3)
+    def _():
+        send_result(2)
 
     def block(which, first, key_row):
         keys = k_ref[pl.ds(key_row, piece), :]
@@ -268,28 +388,88 @@
         lax.fori_loop(0, index, body, 0)
         for g in range(group):
             total = jnp.sum(run_sum[g], axis=1, keepdims=True)
-            o_ref[pl.ds(which * piece, piece), g * HEAD_DIM:(g + 1) * HEAD_DIM] = (acc[g] / total).astype(BF16)
-
-
-def attention(q, kv):
+            o_buf[head, which * piece:(which + 1) * piece, g * HEAD_DIM:(g + 1) * HEAD_DIM] = (acc[g] / total).astype(BF16)
+
+    @pl.when(head == n_heads - 1)
+    def _():
+        for rel in range(2):
+            second(rel).wait_recv()
+            pass_on(rel, 1 - rel)
+        send_result(n_heads - 1)
+        relay_across(2, 0)
+        relay_across(2, 1)
+        relay_across(0, 1)
+        relay_across(1, 0)
+        for rel in range(3):
+            for which in range(2):
+                for from_cp in (False, True):
+                    relay(rel, which, from_cp).wait()
+                across(rel, which).wait_send()
+        for which in range(2):
+            forward(which).wait_send()
+            second(which).wait_send()
+        for h in range(n_heads):
+            copies, local = result_copies(h)
+            for copy in copies + [local]:
+                copy.wait()
+
+
+def attention(q, kv, w_o, w_far, cp_size):
     rows = q.shape[0]
     piece = rows // 2
     kv_heads = kv.shape[1] // (2 * HEAD_DIM)
     group = q.shape[1] // HEAD_DIM // kv_heads
     n_pieces = kv.shape[0] // piece
+    any_spec = pl.BlockSpec(memory_space=pl.ANY)
+    dma = pltpu.SemaphoreType.DMA
     return pl.pallas_call(
-        functools.partial(attention_kernel, n_pieces, group, piece),
+        functools.partial(attention_kernel, n_pieces, group, piece, cp_size),
         grid=(kv_heads,),
         in_specs=[pl.BlockSpec((rows, group * HEAD_DIM), lambda h: (0, h)),
                   pl.BlockSpec((kv.shape[0], HEAD_DIM), lambda h: (0, h)),
-                  pl.BlockSpec((kv.shape[0], HEAD_DIM), lambda h: (0, kv_heads + h))],
-        out_specs=pl.BlockSpec((rows, group * HEAD_DIM), lambda h: (0, h)),
-        out_shape=jax.ShapeDtypeStruct(q.shape, BF16),
-        scratch_shapes=[pltpu.VMEM((group, piece, HEAD_DIM), F32)] * 3,
-        compiler_params=pltpu.CompilerParams(vmem_limit_bytes=48 * 1024 * 1024),
+                  pl.BlockSpec((kv.shape[0], HEAD_DIM), lambda h: (0, kv_heads + h)),
+                  any_spec, any_spec],
+        out_specs=(any_spec, any_spec, any_spec),
+        out_shape=(jax.ShapeDtypeStruct((rows // 4, q.shape[1]), BF16),
+                   jax.ShapeDtypeStruct((3, rows // 4, q.shape[1]), BF16),
+                   jax.ShapeDtypeStruct(w_far.shape, BF16)),
+        scratch_shapes=[pltpu.VMEM((group, piece, HEAD_DIM), F32)] * 3 + [
+            pltpu.VMEM((kv_heads, rows, group * HEAD_DIM), BF16),
+            dma((4,)), dma((4,)), dma((3, 2)), dma((3, 2)), dma((2, 3, 2)), dma((2, 3, 2)),
+            dma((kv_heads, 3)), dma((kv_heads, 3)), dma((kv_heads,)),
+        ],
+        input_output_aliases={4: 2},
+        compiler_params=pltpu.CompilerParams(collective_id=1, has_side_effects=True, vmem_limit_bytes=48 * 1024 * 1024,
+                                             dimension_semantics=("arbitrary",)),
         cost_estimate=pl.CostEstimate(flops=40_000_000_000, bytes_accessed=22_000_000, transcendentals=36_000_000),
         name="attention",
-    )(q, kv, kv)
+    )(q, kv, kv, w_o, w_far)
+
+
+def output_kernel(own_ref, far_ref, wo_ref, w_far_ref, y_ref):
+    total = jnp.dot(own_ref[...], wo_ref[...], preferred_element_type=F32)
+    for rel in range(3):
+        total = total + jnp.dot(far_ref[rel], w_far_ref[rel], preferred_element_type=F32)
+    y_ref[...] = total.astype(BF16)
+
+
+def output_project(own, far, w_o, w_far):
+    rows, depth = own.shape
+    width = w_o.shape[1]
+    tile = 768
+    return pl.pallas_call(
+        output_kernel,
+        grid=(width // tile,),
+        in_specs=[pl.BlockSpec((rows, depth), lambda n: (0, 0)),
+                  pl.BlockSpec((3, rows, depth), lambda n: (0, 0, 0)),
+                  pl.BlockSpec((depth, tile), lambda n: (0, n)),
+                  pl.BlockSpec((3, depth, tile), lambda n: (0, 0, n))],
+        out_specs=pl.BlockSpec((rows, tile), lambda n: (0, n)),
+        out_shape=jax.ShapeDtypeStruct((rows, width), BF16),
+        compiler_params=pltpu.CompilerParams(vmem_limit_bytes=48 * 1024 * 1024),
+        cost_estimate=pl.CostEstimate(flops=8 * rows * depth * width, bytes_accessed=8 * depth * width, transcendentals=0),
+        name="output_project",
+    )(own, far, w_o, w_far)
 
 
 def solution(mesh):
@@ -297,13 +477,8 @@
     row_spec = P(("dp", "cp", "tp"), None)
 
     def local_layer(x_loc, w_q, w_k, w_v, w_o):
-        q, kv = gather_project(x_loc, w_q, w_k, w_v, cp_size)
-        share = w_o.shape[0] // cp_size
-        w_slice = lax.dynamic_slice_in_dim(w_o, lax.axis_index("cp") * share, share, axis=0)
-        w_slice, kv = lax.optimization_barrier((w_slice, kv))
-        w_full = lax.all_gather(w_slice, ("tp", "cp"), axis=0, tiled=True)
-        attn = attention(q, kv)
-        attn_rows = lax.all_to_all(attn, "tp", split_axis=0, concat_axis=1, tiled=True)
-        return jnp.dot(attn_rows, w_full, preferred_element_type=F32).astype(BF16)
+        q, kv, w_far = gather_project(x_loc, w_q, w_k, w_v, w_o, cp_size)
+        own, far, w_far = attention(q, kv, w_o, w_far, cp_size)
+        return output_project(own, far, w_o, w_far)
 
     return jax.shard_map(local_layer, mesh=mesh, in_specs=(row_spec, P(None, "tp"), P(None, "tp"), P(None, "tp"), P("tp", None)), out_specs=row_spec, check_vma=False)

time: 319 us -> 254 us (0.80)
  Pallas kernels: 190 us -> 252 us
  blocking collectives: 52.6 us -> 0 us
  waiting for transfers between devices: 36.9 us -> 0 us
  matrix products: 19.6 us -> 0 us
  between operations: 13.4 us -> 0.03 us
  local copies, waits for them, and re-layouts: 6.68 us -> 1.58 us
    all_to_all x1 -> x0, blocking collectives: 52.6 us -> none  [local_layer(): lax.all_to_all(attn, 'tp', split_axis=0, concat_axis=1, tiled=True)]
    pallas_call x1, Pallas kernels: 64.5 us -> 104 us  [attention(): pl.pallas_call(functools.partial(attention_kernel, n_pieces, group, piece...]
    all_gather x1 -> x0, waiting for transfers between devices: 36.8 us -> none  [local_layer(): w_full = lax.all_gather(w_slice, ('tp', 'cp'), axis=0, tiled=True)]
    pallas_call x0 -> x1, Pallas kernels: none -> 20.3 us  [output_project(): pl.pallas_call(output_kernel, grid=(width // tile,), in_specs=[pl.BlockSp...]
    dot_general x1 -> x0, matrix products: 19.6 us -> none  [local_layer(): return jnp.dot(attn_rows, w_full, preferred_element_type=F32).astype(BF16)]
  transfers between devices with their start and end apart: 1 -> 0, of which waited for: 1 -> 0; matrix products, arithmetic and copies ran while one was open for 1% -> 0% of each run, Pallas kernels for 20% -> 0%
where the time goes in v2:
time: 254 us; the launch traced here: 253 us
  Pallas kernels  252 us (99%)
    pallas_call x1, Pallas kernels, gather_project(): pl.pallas_call(functools.partial(gather_project_kernel, cp_size), out_sha...  127 us
    pallas_call x1, Pallas kernels, attention(): pl.pallas_call(functools.partial(attention_kernel, n_pieces, group, piece...  104 us
    pallas_call x1, Pallas kernels, output_project(): pl.pallas_call(output_kernel, grid=(width // tile,), in_specs=[pl.BlockSp...  20.3 us

profile of v2, /device:TPU:97, one launch (start us, length us, event | category | flops | bytes accessed | tf_op | source)
XLA Modules:
  0.0 253.5 jit_solution(6173942852594048896)
XLA Ops:
  0.0 127.3 %gather_project.1 = (bf16[1024,1024]{1,0:T(8,128)(2,1)}, bf16[8192,1024]{1,0:T(8,128)(2,1)}, bf16[3,1024,5376]{2,1,0:T(8,128)(2,1)}) custom-call(bf16[256,5376]{1,0:T(8,128)(2,1)} %x_ref.1, bf16[5376,1024]{1,0:T(8,128)(2,1)} %wq_ref.1, bf16[5376,512]{1,0:T(8,128)(2,1)} %wk_ref.1, bf16[5376,512]{1,0:T(8,128)(2,1)} %wv_ref.1, bf16[1024,5376]{1,0:T(8,128)(2,1)} %wo_ref.5), custom_call_target="tpu_custom_call" | custom-call | flops 22548578304 | bytes 80000000 | tf_op jit(solution)/shard_map/gather_project/pallas_call | solution.py:221
  127.3 0.0 copy-start
  127.3 1.6 copy-done
  128.9 104.2 %attention.1 = (bf16[256,1024]{1,0:T(8,128)(2,1)S(1)}, bf16[3,256,1024]{2,1,0:T(8,128)(2,1)S(1)}, bf16[3,1024,5376]{2,1,0:T(8,128)(2,1)}) custom-call(bf16[1024,1024]{1,0:T(8,128)(2,1)S(1)} %copy-done, bf16[8192,1024]{1,0:T(8,128)(2,1)} %get-tuple-element.12.k_ref.v_ref, ...), custom_call_target="tpu_custom_call", output_to_operand_aliasing={{2}: (4, {})} | custom-call | flops 40000000000 | bytes 22000000 | tf_op jit(solution)/shard_map/attention/pallas_call | solution.py:425
  233.2 20.3 %output_project.1 = bf16[256,5376]{1,0:T(8,128)(2,1)} custom-call(bf16[256,1024]{1,0:T(8,128)(2,1)S(1)} %get-tuple-element.14.own_ref, bf16[3,256,1024]{2,1,0:T(8,128)(2,1)S(1)} %get-tuple-element.15.far_ref, bf16[1024,5376]{1,0:T(8,128)(2,1)} %wo_ref.5, bf16[3,1024,5376]{2,1,0:T(8,128)(2,1)} %get-tuple-element.16.w_far_ref), custom_call_target="tpu_custom_call" | custom-call | flops 11274289152 | bytes 44040192 | tf_op jit(solution)/shard_map/output_project/pallas_call | solution.py:460
Async XLA Ops:
  127.3 1.6 copy-start

commit v3 on v2

--- a/solution.py
+++ b/solution.py
@@ -137,7 +137,11 @@
         if stage == 0:
             for idx in range(4):
                 loads[1 + idx].wait()
-        lax.fori_loop(0, 4, tile, 0)
+        lax.fori_loop(0, 3, tile, 0)
+        sends = kv_sends(stage)
+        for copy in sends:
+            copy.start()
+        lax.fori_loop(3, 4, tile, 0)
         for part in range(2):
             tp_owner, which = owners[stage][part]
             row = pl.multiple_of(tp_owner * rows + which * half, half)
@@ -149,6 +153,7 @@
             for copy in (q_store, kv_store):
                 copy.start()
                 stores.append(copy)
+        return sends
 
     sent = []
     for stage in range(4):
@@ -162,19 +167,16 @@
         elif stage == 2:
             x_copies[1].wait_recv()
             x_copies[3].wait_recv()
-        else:
-            x_copies[4].wait_recv()
-            x_copies[5].wait_recv()
             wo_copies = [
                 tp_block_copy(wo_ref, wo_out, 0, 0, up_tp, wo_send.at[0], wo_recv.at[0]),
                 tp_block_copy(wo_ref, wo_out, 1, 1, down_tp, wo_send.at[1], wo_recv.at[1]),
             ]
             for copy in wo_copies:
                 copy.start()
-        project(stage)
-        sends = kv_sends(stage)
-        for copy in sends:
-            copy.start()
+        else:
+            x_copies[4].wait_recv()
+            x_copies[5].wait_recv()
+        sends = project(stage)
         if stage > 0:
             for copy in forwards[:2]:
                 copy.wait_recv()
@@ -244,8 +246,9 @@
     )(x_loc, w_q, w_k, w_v, w_o)
 
 
-def attention_kernel(n_pieces, group, q_chunk, cp_size, q_ref, k_ref, v_ref, wo_ref, wo_in, own_out, far_out, wo_out,
-                     acc, run_max, run_sum, o_buf, y_send, y_recv, x_send, x_recv, d_send, d_recv, o_send, o_recv, o_local):
+def attention_kernel(n_pieces, group, q_chunk, cp_size, q_ref, k_ref, v_ref, wo_ref, wo_in, y_ref, wo_out,
+                     acc, run_max, run_sum, o_buf, far_buf, y_acc, w_slots,
+                     y_send, y_recv, x_send, x_recv, d_send, d_recv, o_send, o_recv, w_load):
     del wo_in
     head = pl.program_id(0)
     n_heads = o_buf.shape[0]
@@ -293,16 +296,13 @@
         for rel, target in ((0, up_tp), (1, down_tp), (2, opp_tp)):
             copies.append(pltpu.make_async_remote_copy(
                 src_ref=o_buf.at[h, pl.ds(pl.multiple_of(target * rows, rows), rows), :],
-                dst_ref=far_out.at[rel, :, pl.ds(h * width, width)],
+                dst_ref=far_buf.at[rel, :, pl.ds(h * width, width)],
                 send_sem=o_send.at[h, rel], recv_sem=o_recv.at[h, rel],
                 device_id={"tp": target}, device_id_type=MESH))
-        local = pltpu.make_async_copy(o_buf.at[h, pl.ds(pl.multiple_of(tp_rank * rows, rows), rows), :],
-                                      own_out.at[:, pl.ds(h * width, width)], o_local.at[h])
-        return copies, local
+        return copies
 
     def send_result(h):
-        copies, local = result_copies(h)
-        for copy in copies + [local]:
+        for copy in result_copies(h):
             copy.start()
 
     def pass_on(rel, which):
@@ -390,28 +390,104 @@
             total = jnp.sum(run_sum[g], axis=1, keepdims=True)
             o_buf[head, which * piece:(which + 1) * piece, g * HEAD_DIM:(g + 1) * HEAD_DIM] = (acc[g] / total).astype(BF16)
 
+    quarter = wo_ref.shape[0] // 4
+    near, beyond = parity * 2 * quarter, (1 - parity) * 2 * quarter
+    own_rows = pl.ds(pl.multiple_of(tp_rank * rows, rows), rows)
+    chunks = [
+        ((None, 0), (None, quarter)),
+        ((None, 2 * quarter), (None, 3 * quarter)),
+        ((0, near), (0, near + quarter)),
+        ((1, near), (1, near + quarter)),
+        ((2, near), (2, near + quarter)),
+        ((2, beyond), (2, beyond + quarter)),
+        ((0, beyond), (1, beyond + quarter)),
+        ((0, beyond + quarter), (1, beyond)),
+    ]
+
+    def chunk_loads(idx):
+        slot = idx % 4
+        loads = []
+        for part, (rel, row) in enumerate(chunks[idx]):
+            window = pl.ds(pl.multiple_of(row, quarter), quarter)
+            src = wo_ref.at[window, :] if rel is None else wo_out.at[rel, window, :]
+            loads.append(pltpu.make_async_copy(src, w_slots.at[slot, pl.ds(part * quarter, quarter), :],
+                                               w_load.at[slot, part]))
+        return loads
+
+    def start_loads(idx):
+        for copy in chunk_loads(idx):
+            copy.start()
+
+    def project(*indices):
+        halves = []
+        for idx in indices:
+            for copy in chunk_loads(idx):
+                copy.wait()
+            for rel, row in chunks[idx]:
+                if rel is None:
+                    halves.append(o_buf[row // width, own_rows, :])
+                else:
+                    halves.append(far_buf[rel, :, pl.ds(pl.multiple_of(row, quarter), quarter)])
+        lhs = jnp.concatenate(halves, axis=1)
+        tile = 1792
+        slot = indices[0] % 4
+
+        def step(n, carry):
+            cols = pl.ds(pl.multiple_of(n * tile, tile), tile)
+            rhs = w_slots[slot:slot + len(indices), :, cols].reshape(lhs.shape[1], tile)
+            val = jnp.dot(lhs, rhs, preferred_element_type=F32)
+            if indices[0] > 0:
+                val = y_acc[:, cols] + val
+            if indices[-1] < len(chunks) - 1:
+                y_acc[:, cols] = val
+            else:
+                y_ref[:, cols] = val.astype(BF16)
+            return carry
+
+        lax.fori_loop(0, y_ref.shape[1] // tile, step, 0)
+
     @pl.when(head == n_heads - 1)
     def _():
+        start_loads(0)
+        start_loads(1)
         for rel in range(2):
             second(rel).wait_recv()
             pass_on(rel, 1 - rel)
         send_result(n_heads - 1)
         relay_across(2, 0)
         relay_across(2, 1)
+        project(0, 1)
+        for rel in range(3):
+            for which in range(2):
+                relay(rel, which, False).wait_recv()
+                if rel == 2 or which == rel:
+                    relay(rel, which, True).wait_recv()
+        for idx in range(2, 6):
+            start_loads(idx)
+        for h in range(n_heads):
+            for copy in result_copies(h):
+                copy.wait_recv()
+        project(2, 3)
+        start_loads(6)
+        project(4, 5)
+        project(6)
         relay_across(0, 1)
         relay_across(1, 0)
+        relay(0, 1, True).wait_recv()
+        relay(1, 0, True).wait_recv()
+        start_loads(7)
+        project(7)
         for rel in range(3):
             for which in range(2):
                 for from_cp in (False, True):
-                    relay(rel, which, from_cp).wait()
+                    relay(rel, which, from_cp).wait_send()
                 across(rel, which).wait_send()
         for which in range(2):
             forward(which).wait_send()
             second(which).wait_send()
         for h in range(n_heads):
-            copies, local = result_copies(h)
-            for copy in copies + [local]:
-                copy.wait()
+            for copy in result_copies(h):
+                copy.wait_send()
 
 
 def attention(q, kv, w_o, w_far, cp_size):
@@ -429,56 +505,30 @@
                   pl.BlockSpec((kv.shape[0], HEAD_DIM), lambda h: (0, h)),
                   pl.BlockSpec((kv.shape[0], HEAD_DIM), lambda h: (0, kv_heads + h)),
                   any_spec, any_spec],
-        out_specs=(any_spec, any_spec, any_spec),
-        out_shape=(jax.ShapeDtypeStruct((rows // 4, q.shape[1]), BF16),
-                   jax.ShapeDtypeStruct((3, rows // 4, q.shape[1]), BF16),
-                   jax.ShapeDtypeStruct(w_far.shape, BF16)),
+        out_specs=(pl.BlockSpec((rows // 4, w_o.shape[1]), lambda h: (0, 0)), any_spec),
+        out_shape=(jax.ShapeDtypeStruct((rows // 4, w_o.shape[1]), BF16), jax.ShapeDtypeStruct(w_far.shape, BF16)),
         scratch_shapes=[pltpu.VMEM((group, piece, HEAD_DIM), F32)] * 3 + [
             pltpu.VMEM((kv_heads, rows, group * HEAD_DIM), BF16),
+            pltpu.VMEM((3, rows // 4, q.shape[1]), BF16),
+            pltpu.VMEM((rows // 4, w_o.shape[1]), F32),
+            pltpu.VMEM((4, w_o.shape[0] // 2, w_o.shape[1]), BF16),
             dma((4,)), dma((4,)), dma((3, 2)), dma((3, 2)), dma((2, 3, 2)), dma((2, 3, 2)),
-            dma((kv_heads, 3)), dma((kv_heads, 3)), dma((kv_heads,)),
+            dma((kv_heads, 3)), dma((kv_heads, 3)), dma((4, 2)),
         ],
-        input_output_aliases={4: 2},
-        compiler_params=pltpu.CompilerParams(collective_id=1, has_side_effects=True, vmem_limit_bytes=48 * 1024 * 1024,
+        input_output_aliases={4: 1},
+        compiler_params=pltpu.CompilerParams(collective_id=1, has_side_effects=True, vmem_limit_bytes=VMEM_LIMIT,
                                              dimension_semantics=("arbitrary",)),
         cost_estimate=pl.CostEstimate(flops=40_000_000_000, bytes_accessed=22_000_000, transcendentals=36_000_000),
         name="attention",
     )(q, kv, kv, w_o, w_far)
 
 
-def output_kernel(own_ref, far_ref, wo_ref, w_far_ref, y_ref):
-    total = jnp.dot(own_ref[...], wo_ref[...], preferred_element_type=F32)
-    for rel in range(3):
-        total = total + jnp.dot(far_ref[rel], w_far_ref[rel], preferred_element_type=F32)
-    y_ref[...] = total.astype(BF16)
-
-
-def output_project(own, far, w_o, w_far):
-    rows, depth = own.shape
-    width = w_o.shape[1]
-    tile = 768
-    return pl.pallas_call(
-        output_kernel,
-        grid=(width // tile,),
-        in_specs=[pl.BlockSpec((rows, depth), lambda n: (0, 0)),
-                  pl.BlockSpec((3, rows, depth), lambda n: (0, 0, 0)),
-                  pl.BlockSpec((depth, tile), lambda n: (0, n)),
-                  pl.BlockSpec((3, depth, tile), lambda n: (0, 0, n))],
-        out_specs=pl.BlockSpec((rows, tile), lambda n: (0, n)),
-        out_shape=jax.ShapeDtypeStruct((rows, width), BF16),
-        compiler_params=pltpu.CompilerParams(vmem_limit_bytes=48 * 1024 * 1024),
-        cost_estimate=pl.CostEstimate(flops=8 * rows * depth * width, bytes_accessed=8 * depth * width, transcendentals=0),
-        name="output_project",
-    )(own, far, w_o, w_far)
-
-
 def solution(mesh):
     cp_size = mesh.shape["cp"]
     row_spec = P(("dp", "cp", "tp"), None)
 
     def local_layer(x_loc, w_q, w_k, w_v, w_o):
         q, kv, w_far = gather_project(x_loc, w_q, w_k, w_v, w_o, cp_size)
-        own, far, w_far = attention(q, kv, w_o, w_far, cp_size)
-        return output_project(own, far, w_o, w_far)
+        return attention(q, kv, w_o, w_far, cp_size)[0]
 
     return jax.shard_map(local_layer, mesh=mesh, in_specs=(row_spec, P(None, "tp"), P(None, "tp"), P(None, "tp"), P("tp", None)), out_specs=row_spec, check_vma=False)

time: 254 us -> 241 us (0.949)
  Pallas kernels: 252 us -> 237 us
    pallas_call x1 -> x0, Pallas kernels: 20.3 us -> none  [output_project(): pl.pallas_call(output_kernel, grid=(width // tile,), in_specs=[pl.BlockSp...]
    pallas_call x1, Pallas kernels: 104 us -> 109 us  [attention(): pl.pallas_call(functools.partial(attention_kernel, n_pieces, group, piece...]
where the time goes in v3:
time: 241 us
  Pallas kernels  237 us (98%)
  local copies, waits for them, and re-layouts  3.49 us (1%)
    pallas_call x1, Pallas kernels, gather_project(): pl.pallas_call(functools.partial(gather_project_kernel, cp_size), out_sha...  128 us
    pallas_call x1, Pallas kernels, attention(): pl.pallas_call(functools.partial(attention_kernel, n_pieces, group, piece...  109 us

profile of v3, /device:TPU:97, one launch (start us, length us, event | category | flops | bytes accessed | tf_op | source)
XLA Modules:
  0.0 240.6 jit_solution(15682885319725111631)
XLA Ops:
  0.0 127.8 %gather_project.1 = (bf16[1024,1024]{1,0:T(8,128)(2,1)}, bf16[8192,1024]{1,0:T(8,128)(2,1)}, bf16[3,1024,5376]{2,1,0:T(8,128)(2,1)}) custom-call(bf16[256,5376]{1,0:T(8,128)(2,1)} %x_ref.1, bf16[5376,1024]{1,0:T(8,128)(2,1)} %wq_ref.1, bf16[5376,512]{1,0:T(8,128)(2,1)} %wk_ref.1, bf16[5376,512]{1,0:T(8,128)(2,1)} %wv_ref.1, bf16[1024,5376]{1,0:T(8,128)(2,1)} %wo_ref.3), custom_call_target="tpu_custom_call" | custom-call | flops 22548578304 | bytes 80000000 | tf_op jit(solution)/shard_map/gather_project/pallas_call | solution.py:223
  127.8 109.3 %attention.1 = (bf16[256,5376]{1,0:T(8,128)(2,1)}, bf16[3,1024,5376]{2,1,0:T(8,128)(2,1)}) custom-call(bf16[1024,1024]{1,0:T(8,128)(2,1)} %get-tuple-element.9.q_ref, bf16[8192,1024]{1,0:T(8,128)(2,1)} %get-tuple-element.10.k_ref.v_ref, bf16[8192,1024]{1,0:T(8,128)(2,1)} %get-tuple-element.10.k_ref.v_ref, ...), custom_call_target="tpu_custom_call", output_to_operand_aliasing={{1}: (4, {})} | custom-call | flops 40000000000 | bytes 22000000 | tf_op jit(solution)/shard_map/attention/pallas_call | solution.py:501
  237.1 3.5 %copy.9 = bf16[256,5376]{1,0:T(8,128)(2,1)} copy(bf16[256,5376]{1,0:T(8,128)(2,1)} %get-tuple-element.12) | data formatting | bytes 5505024
